TPU v7x, 128 devices: a whole 4x4x4 slice. The times are simulated.
128 devices in a mesh: dp: 1, col: 2 (over core), row: 64 (over z, y, x).
Axes of the slice: x: 4, y: 4, z: 4, core: 2. Of those that a mesh axis runs over, the one named last changes fastest.
Arguments:
- x_tok: bfloat16 [131072, 2048], P(('dp', 'row'), 'col')
- ln_gamma: float32 [2048], P('col')
- w_in: bfloat16 [2048, 8192], P('row', 'col')
- w_out: bfloat16 [8192, 2048], P('row', 'col')
Outputs:
- output: bfloat16 [131072, 2048], P(('dp', 'row'), 'col')
All inputs are finite; a program needn't handle non-finite values.
Results may differ from a plain program's by a relative error of at most 0.00102.
Values are sent between devices in bfloat16 or wider.
A program may use at most 1 GiB of HBM per device.

v0:
```python
import jax
import jax.numpy as jnp
from jax import lax
from jax.sharding import PartitionSpec as P

LN_EPS = 1e-5


def solution(mesh):
    col_size = mesh.shape["col"]
    tok_spec = P(("dp", "row"), "col")

    def local_block(x_loc, gamma_loc, w_in_loc, w_out_loc):
        d_model = x_loc.shape[1] * col_size
        x_f32 = x_loc.astype(jnp.float32)
        part_sums = jnp.concatenate([jnp.sum(x_f32, axis=1, keepdims=True), jnp.sum(x_f32 * x_f32, axis=1, keepdims=True)], axis=1)
        row_sums = lax.psum(part_sums, "col")
        mean_row = row_sums[:, 0:1] / d_model
        var_row = row_sums[:, 1:2] / d_model - mean_row * mean_row
        normed = ((x_f32 - mean_row) * lax.rsqrt(var_row + LN_EPS) * gamma_loc).astype(jnp.bfloat16)
        z_panel = lax.all_gather(normed, "col", axis=1, tiled=True)
        w_in_panel = lax.all_gather(w_in_loc, "row", axis=0, tiled=True)
        pre_act = jnp.dot(z_panel, w_in_panel, preferred_element_type=jnp.float32)
        hidden = jax.nn.gelu(pre_act, approximate=True).astype(jnp.bfloat16)
        h_panel = lax.all_gather(hidden, "col", axis=1, tiled=True)
        w_out_panel = lax.all_gather(w_out_loc, "row", axis=0, tiled=True)
        branch = jnp.dot(h_panel, w_out_panel, preferred_element_type=jnp.float32)
        return (x_f32 + branch).astype(jnp.bfloat16)

    return jax.shard_map(local_block, mesh=mesh, in_specs=(tok_spec, P("col"), P("row", "col"), P("row", "col")), out_specs=tok_spec, check_vma=False)
```

profile of v0, /device:TPU:0, one launch (start us, length us, event | category | flops | bytes accessed | tf_op | source)
XLA Modules:
  0.0 364.4 jit_solution(5268605466039881281)
XLA Ops:
  6.5 0.0 all-gather.5.cloned.1.call-start
  6.5 3.4 convert_reduce_fusion
  10.0 3.4 psum.7
  13.4 4.3 %fusion.11 = bf16[2048,1024]{1,0:T(8,128)(2,1)} fusion(bf16[2048,1024]{1,0:T(8,128)(2,1)} %param.4, f32[1024]{0:T(1024)} %param.5, f32[2048]{0:T(1024)S(1)} %bitcast.11, f32[2048]{0:T(1024)S(1)} %bitcast.10), kind=kLoop, calls=%fused_computation.16 | loop fusion | flops 10485760 | bytes 8409088 | tf_op jit(solution)/shard_map/convert_element_type | solution.py:20
  17.7 0.0 all-gather.5.cloned.1.call-update
  17.7 0.0 all-gather.7.cloned.1.call-start
  17.8 0.7 all-gather.7.cloned.1.call-update
  18.5 0.0 all-gather.11.cloned.1.call-start
  18.5 0.7 all-gather.11.cloned.1.call-update
  19.2 0.2 all-gather.9.cloned.1.call-start
  19.4 24.4 %all-gather.5.cloned.1.call-done = bf16[2048,2048]{1,0:T(8,128)(2,1)} async-done(((bf16[2048,1024]{1,0:T(8,128)(2,1)}), bf16[2048,2048]{1,0:T(8,128)(2,1)}) %all-gather.5.cloned.1.call-update) | async-done | bytes 8388624 | tf_op jit(solution)/shard_map/all_gather | solution.py:21
  43.9 108.2 %all-gather.7.cloned.1.call-done = bf16[2048,4096]{1,0:T(8,128)(2,1)} async-done(((bf16[32,4096]{1,0:T(8,128)(2,1)}), bf16[2048,4096]{1,0:T(8,128)(2,1)}) %all-gather.7.cloned.1.call-update) | async-done | bytes 16777232 | tf_op jit(solution)/shard_map/all_gather | solution.py:22
  152.1 49.8 %fusion.7 = bf16[2048,4096]{1,0:T(8,128)(2,1)} fusion(bf16[2048,2048]{1,0:T(8,128)(2,1)} %all-gather.5.cloned.1.call-done, bf16[2048,4096]{1,0:T(8,128)(2,1)} %all-gather.7.cloned.1.call-done), kind=kOutput, calls=%fused_computation.8 | convolution fusion | flops 34435235840 | bytes 41943040 | tf_op jit(solution)/shard_map/dot_general | solution.py:23
  201.9 0.0 all-gather.9.cloned.1.call-update
  201.9 56.6 %all-gather.11.cloned.1.call-done = bf16[8192,1024]{1,0:T(8,128)(2,1)} async-done(((bf16[128,1024]{1,0:T(8,128)(2,1)}), bf16[8192,1024]{1,0:T(8,128)(2,1)}) %all-gather.11.cloned.1.call-update) | async-done | bytes 16777232 | tf_op jit(solution)/shard_map/all_gather | solution.py:26
  258.5 54.7 %all-gather.9.cloned.1.call-done = bf16[2048,8192]{1,0:T(8,128)(2,1)} async-done(((bf16[2048,4096]{1,0:T(8,128)(2,1)}), bf16[2048,8192]{1,0:T(8,128)(2,1)}) %all-gather.9.cloned.1.call-update) | async-done | bytes 33554448 | tf_op jit(solution)/shard_map/all_gather | solution.py:25
  313.2 44.7 %fusion.12 = bf16[2048,1024]{1,0:T(8,128)(2,1)} fusion(bf16[2048,1024]{1,0:T(8,128)(2,1)} %param.4, bf16[2048,8192]{1,0:T(8,128)(2,1)} %all-gather.9.cloned.1.call-done, bf16[8192,1024]{1,0:T(8,128)(2,1)} %all-gather.11.cloned.1.call-done), kind=kOutput, calls=%fused_computation.17 | convolution fusion | flops 34366029824 | bytes 58720256 | tf_op jit(solution)/shard_map/dot_general | solution.py:27
  (2 shorter events, 0.0 us)
Async XLA Ops:
  6.5 37.3 %all-gather.5.cloned.1.call-start = ((), (), s32[]{:S(2)}) async-start(), calls=%async_computation | async-start | bytes 12582912 | tf_op jit(solution)/shard_map/all_gather | solution.py:21
  17.7 134.4 %all-gather.7.cloned.1.call-start = ((), (), s32[]{:S(2)}) async-start(), calls=%async_computation.1 | async-start | bytes 17039360 | tf_op jit(solution)/shard_map/all_gather | solution.py:22
  18.5 240.1 %all-gather.11.cloned.1.call-start = ((), (), s32[]{:S(2)}) async-start(), calls=%async_computation.3 | async-start | bytes 17039360 | tf_op jit(solution)/shard_map/all_gather | solution.py:26
  19.2 294.0 %all-gather.9.cloned.1.call-start = ((), (), s32[]{:S(2)}) async-start(), calls=%async_computation.2 | async-start | bytes 50331648 | tf_op jit(solution)/shard_map/all_gather | solution.py:25
Sparse Core Ops, SparseCore 0:
  17.8 25.9 all-gather.4
  46.8 105.2 all-gather.6
  155.0 103.4 all-gather.10
  260.0 53.1 all-gather.8
where the time goes:
time: 366 us; the launch traced here: 364 us
  waiting for transfers between devices  245 us (67%)
  matrix products  94.5 us (26%)
  between operations  13.1 us (4%)
  other arithmetic  7.78 us (2%)
    all_gather x1, waiting for transfers between devices, local_block(): w_in_panel = lax.all_gather(w_in_loc, 'row', axis=0, tiled=True)  108 us
    all_gather x1, waiting for transfers between devices, local_block(): w_out_panel = lax.all_gather(w_out_loc, 'row', axis=0, tiled=True)  56.6 us
    all_gather x1, waiting for transfers between devices, local_block(): h_panel = lax.all_gather(hidden, 'col', axis=1, tiled=True)  54.7 us
    dot_general x1, matrix products, local_block(): pre_act = jnp.dot(z_panel, w_in_panel, preferred_element_type=jnp.float32)  49.8 us
    dot_general x1, matrix products, local_block(): branch = jnp.dot(h_panel, w_out_panel, preferred_element_type=jnp.float32)  44.7 us
    all_gather x1, waiting for transfers between devices, local_block(): z_panel = lax.all_gather(normed, 'col', axis=1, tiled=True)  24.4 us
  transfers between devices with their start and end apart: 4, of which 4 were waited for; matrix products, arithmetic and copies ran while one was open for 14% of the time, Pallas kernels for 0%

commit v1 on v0

v1 whole, which is shorter than its diff:
```python
import functools

import jax
import jax.numpy as jnp
from jax import lax
from jax.experimental import pallas as pl
from jax.experimental.pallas import tpu as pltpu
from jax.sharding import PartitionSpec as P

LN_EPS = 1e-5
GELU_C = 0.7978845608028654
MESH = pl.DeviceIdType.MESH
BF16 = jnp.bfloat16
F32 = jnp.float32

NU = 32
NH = 16
UR, UC = 32, 256
ORDERS = (("x", "y", "z"), ("y", "z", "x"), ("z", "x", "y"))
NS = 11
TOK = 2048
DM = 2048
HALF = 1024
MT = 1024
SLOTS = 6


def gelu(a):
    return 0.5 * a * (1.0 + jnp.tanh(GELU_C * (a + 0.044715 * (a * a * a))))


def kernel(x_ref, g_ref, w1_ref, w2_ref, y_ref, w_ref, z, h, wbuf, wsh, s1, perm, gbuf, acc, xres, ybuf,
           recv_sem, send_sem, h_recv, h_send, load_sem, loc_sem, x_recv, x_send, io_sem):
    me = lax.axis_index("row")
    c = lax.axis_index("col")
    pos = {"x": lax.rem(me, 4), "y": lax.rem(me // 4, 4), "z": me // 16}
    stride = {"x": 1, "y": 4, "z": 16}

    def shifted(d, k):
        return lax.rem(pos[d] + (k + 4), 4)

    peer = {(d, k): me + (shifted(d, k) - pos[d]) * stride[d] for d in "xyz" for k in (1, -1)}

    def region(u, p, k, at, half):
        dims = ORDERS[p]
        idx = {}
        for j, d in enumerate(dims):
            idx[d] = pl.ds(0, 4) if j < k else (at if j == k else pos[d])
        rows = pl.ds(0, UR)
        if half is not None:
            if k == 0:
                rows = pl.ds(half * (UR // 2), UR // 2)
            else:
                d = [d for d in "zyx" if d in dims[:k]][0]
                idx[d] = pl.ds(2 * half, 2)
        return w_ref.at[u, idx["z"], idx["y"], idx["x"], rows]

    def bytes_of(u, k, n):
        return (w_ref.at[u, 0, 0, pl.ds(0, n)], w_ref.at[u, 0, pl.ds(0, n)], w_ref.at[u, pl.ds(0, n)])[k]

    def send(u, p, k, sub, way):
        d = ORDERS[p][k]
        if sub == 0:
            dst = region(u, p, k, pos[d], None)
            src = wsh.at[u] if k == 0 else dst
        else:
            dst = region(u, p, k, shifted(d, -way), 0 if way == 1 else 1)
            src = dst
        pltpu.make_async_remote_copy(
            src_ref=src, dst_ref=dst, send_sem=send_sem.at[u, k], recv_sem=recv_sem.at[u, k, sub],
            device_id={"row": peer[d, way]}, device_id_type=MESH).start()

    def wait_recv(u, k, sub):
        v = bytes_of(u, k, 2 if sub == 0 else 1)
        pltpu.make_async_copy(v, v, recv_sem.at[u, k, sub]).wait()

    def each(s, f):
        for p in range(3):
            u = 3 * s + p
            if isinstance(s, int):
                if 0 <= s and u < NU:
                    f(u, p)
            else:
                pl.when(jnp.logical_and(s >= 0, u < NU))(functools.partial(f, u, p))

    def issue(s, k, sub):
        def f(u, p):
            send(u, p, k, sub, 1)
            send(u, p, k, sub, -1)
        each(s, f)

    def await_(s, k, sub):
        each(s, lambda u, p: wait_recv(u, k, sub))

    cp_w1 = pltpu.make_async_copy(w1_ref, s1, io_sem.at[0])
    cp_w1.start()
    cp_w2 = [pltpu.make_async_copy(w2_ref.at[pl.ds(UR * rg, UR), pl.ds(UC * cg, UC)], wsh.at[NH + 4 * cg + rg], io_sem.at[1])
             for cg in range(4) for rg in range(4)]
    for cp in cp_w2:
        cp.start()
    mine = pl.ds(pl.multiple_of(c * HALF, HALF), HALF)
    cp_x = pltpu.make_async_copy(x_ref, z.at[:, mine], io_sem.at[2])
    cp_x.start()
    cp_g = pltpu.make_async_copy(g_ref, gbuf.at[c], io_sem.at[3])
    cp_g.start()

    barrier = pltpu.get_barrier_semaphore()
    for t in peer.values():
        pl.semaphore_signal(barrier, inc=1, device_id={"row": t}, device_id_type=MESH)
    pl.semaphore_signal(barrier, inc=1, device_id={"col": 1 - c}, device_id_type=MESH)

    ri = lax.broadcasted_iota(jnp.int32, (512, 512), 0)
    ci = lax.broadcasted_iota(jnp.int32, (512, 512), 1)
    want = ((ci // 32) % 4) * 128 + (ci // 128) * 32 + ci % 32
    perm[...] = jnp.where(ri == want, 1.0, 0.0).astype(BF16)
    cp_w1.wait()
    for g in range(8):
        r = jnp.dot(s1[:, g * 512:(g + 1) * 512], perm[...], preferred_element_type=F32).astype(BF16)
        for rg in range(4):
            wsh[4 * rg + g // 2, :, (g % 2) * 128:(g % 2) * 128 + 128] = r[:, rg * 128:(rg + 1) * 128]
    pl.semaphore_wait(barrier, 7)

    other = {"col": 1 - c}
    rx = pltpu.make_async_remote_copy(src_ref=x_ref, dst_ref=z.at[:, mine], send_sem=x_send.at[0], recv_sem=x_recv.at[0],
                                      device_id=other, device_id_type=MESH)
    rx.start()
    rg_ = pltpu.make_async_remote_copy(src_ref=g_ref, dst_ref=gbuf.at[c], send_sem=x_send.at[1], recv_sem=x_recv.at[1],
                                       device_id=other, device_id_type=MESH)
    rg_.start()
    pltpu.make_async_copy(wsh.at[pl.ds(NH, NH)], wsh.at[pl.ds(NH, NH)], io_sem.at[1]).wait()
    for s in range(5):
        issue(s, 0, 0)
    own = pltpu.make_async_copy(wsh, w_ref.at[:, pos["z"], pos["y"], pos["x"]], loc_sem)
    own.start()
    for s in range(4):
        await_(s, 0, 0)
        issue(s, 0, 1)
    own.wait()
    for s in range(3):
        await_(s, 0, 1)
        issue(s, 1, 0)
    for s in range(2):
        await_(s, 1, 0)
        issue(s, 1, 1)
    await_(0, 1, 1)
    issue(0, 2, 0)

    def norm():
        cp_x.wait()
        cp_g.wait()
        rx.wait_recv()
        rg_.wait_recv()

        @pl.loop(0, TOK // 128)
        def _(i):
            rows = pl.ds(pl.multiple_of(i * 128, 128), 128)
            a = z[rows, :].astype(F32)
            mean = jnp.sum(a, axis=1, keepdims=True) / DM
            var = jnp.sum(a * a, axis=1, keepdims=True) / DM - mean * mean
            rs = lax.rsqrt(var + LN_EPS)
            for hf in range(2):
                cols = slice(hf * HALF, (hf + 1) * HALF)
                z[rows, cols] = ((a[:, cols] - mean) * rs * gbuf[hf]).astype(BF16)

    def load(u):
        return pltpu.make_async_copy(w_ref.at[u], wbuf.at[lax.rem(u, SLOTS)], load_sem.at[lax.rem(u, SLOTS)])

    def h_copy(u):
        cols = pl.ds(pl.multiple_of(c * HALF + lax.rem(u, 4) * UC, UC), UC)
        v = h.at[u // 4, :, cols]
        return pltpu.make_async_remote_copy(src_ref=v, dst_ref=v, send_sem=h_send.at[u], recv_sem=h_recv.at[u],
                                            device_id=other, device_id_type=MESH)

    def out_copy(cg):
        return pltpu.make_async_copy(ybuf, y_ref.at[:, pl.ds(pl.multiple_of(cg * UC, UC), UC)], io_sem.at[4])

    def res_copy(cg):
        return pltpu.make_async_copy(x_ref.at[:, pl.ds(pl.multiple_of(cg * UC, UC), UC)], xres, io_sem.at[5])

    def compute(u):
        slot = lax.rem(u, SLOTS)
        load(u).wait()

        @pl.when(u < NH)
        def _():
            cols = pl.ds(pl.multiple_of(c * HALF + lax.rem(u, 4) * UC, UC), UC)

            @pl.loop(0, TOK // MT)
            def _(m):
                rows = pl.ds(pl.multiple_of(m * MT, MT), MT)
                r = jnp.dot(z[rows, :], wbuf[slot].reshape(DM, UC), preferred_element_type=F32)
                h[u // 4, rows, cols] = gelu(r).astype(BF16)

            h_copy(u).start()

        @pl.when(u >= NH)
        def _():
            cg = (u - NH) // 4
            rg = lax.rem(u, 4)

            @pl.when(rg == 0)
            def _():
                acc[...] = jnp.zeros_like(acc)
                res_copy(cg).start()

            @pl.when(cg == 0)
            def _():
                for q in range(4):
                    h_copy(4 * rg + q).wait_recv()

            @pl.loop(0, TOK // MT)
            def _(m):
                rows = pl.ds(pl.multiple_of(m * MT, MT), MT)
                acc[rows, :] += jnp.dot(h[rg, rows, :], wbuf[slot].reshape(DM, UC), preferred_element_type=F32)

            @pl.when(rg == 3)
            def _():
                res_copy(cg).wait()

                @pl.when(cg > 0)
                def _():
                    out_copy(cg - 1).wait()

                ybuf[...] = (xres[...].astype(F32) + acc[...]).astype(BF16)
                out_copy(cg).start()

    @pl.loop(0, NS + 2)
    def _(s):
        await_(s + 2, 1, 0)
        await_(s + 3, 0, 1)
        await_(s + 4, 0, 0)
        pl.when(s >= 1)(lambda: await_(s - 1, 2, 0))
        issue(s - 1, 2, 1)
        issue(s + 2, 1, 1)
        issue(s + 3, 1, 0)
        issue(s + 4, 0, 1)
        issue(s + 5, 0, 0)
        await_(s + 1, 1, 1)
        issue(s + 1, 2, 0)

        def fetch(u, p):
            wait_recv(u, 2, 1)
            load(u).start()

        each(s - 2, fetch)
        pl.when(s == 0)(norm)
        first = 3 * jnp.maximum(s - 2, 0)
        last = jnp.minimum(3 * jnp.maximum(s - 1, 0), NU)

        @pl.loop(first, last)
        def _(u):
            compute(u)

    out_copy(3).wait()
    rx.wait_send()
    rg_.wait_send()

    @pl.loop(0, NH)
    def _(u):
        h_copy(u).wait_send()

    @pl.loop(0, NU)
    def _(u):
        for k in range(3):
            v = bytes_of(u, k, 3)
            pltpu.make_async_copy(v, v, send_sem.at[u, k]).wait()


def solution(mesh):
    tok_spec = P(("dp", "row"), "col")

    def local_block(x_loc, gamma_loc, w_in_loc, w_out_loc):
        y, _ = pl.pallas_call(
            kernel,
            out_shape=(jax.ShapeDtypeStruct((TOK, HALF), BF16), jax.ShapeDtypeStruct((NU, 4, 4, 4, UR, UC), BF16)),
            in_specs=[pl.BlockSpec(memory_space=pl.ANY)] * 4,
            out_specs=(pl.BlockSpec(memory_space=pl.ANY), pl.BlockSpec(memory_space=pl.ANY)),
            scratch_shapes=[
                pltpu.VMEM((TOK, DM), BF16),
                pltpu.VMEM((4, TOK, DM), BF16),
                pltpu.VMEM((SLOTS, 4, 4, 4, UR, UC), BF16),
                pltpu.VMEM((NU, UR, UC), BF16),
                pltpu.VMEM((UR, 4096), BF16),
                pltpu.VMEM((512, 512), BF16),
                pltpu.VMEM((2, 1, HALF), F32),
                pltpu.VMEM((TOK, UC), F32),
                pltpu.VMEM((TOK, UC), BF16),
                pltpu.VMEM((TOK, UC), BF16),
                pltpu.SemaphoreType.DMA((NU, 3, 2)),
                pltpu.SemaphoreType.DMA((NU, 3)),
                pltpu.SemaphoreType.DMA((NH,)),
                pltpu.SemaphoreType.DMA((NH,)),
                pltpu.SemaphoreType.DMA((SLOTS,)),
                pltpu.SemaphoreType.DMA,
                pltpu.SemaphoreType.DMA((2,)),
                pltpu.SemaphoreType.DMA((2,)),
                pltpu.SemaphoreType.DMA((6,)),
            ],
            compiler_params=pltpu.CompilerParams(collective_id=0, has_side_effects=True, vmem_limit_bytes=67043328),
        )(x_loc, gamma_loc.reshape(1, HALF), w_in_loc, w_out_loc)
        return y

    return jax.shard_map(local_block, mesh=mesh, in_specs=(tok_spec, P("col"), P("row", "col"), P("row", "col")), out_specs=tok_spec, check_vma=False)
```

time: 366 us -> 164 us (0.45)
  waiting for transfers between devices: 245 us -> 0 us
  Pallas kernels: 0 us -> 159 us
  matrix products: 94.5 us -> 0 us
  between operations: 13.1 us -> 0.01 us
  other arithmetic: 7.78 us -> 0 us
  local copies, waits for them, and re-layouts: 0 us -> 4.64 us
    all_gather x4 -> x0, waiting for transfers between devices: 244 us -> none  [the longest x1 108 us: local_block(): w_in_panel = lax.all_gather(w_in_loc, 'row', axis=0, tiled=True)]
    pallas_call x0 -> x1, Pallas kernels: none -> 159 us  [local_block(): pl.pallas_call(kernel, out_shape=(jax.ShapeDtypeStruct((TOK, HALF), BF16)...]
    dot_general x2 -> x0, matrix products: 94.5 us -> none  [the longest x1 49.8 us: local_block(): pre_act = jnp.dot(z_panel, w_in_panel, preferred_element_type=jnp.float32)]
    unnamed x0 -> x1, local copies, waits for them, and re-layouts: none -> 4.64 us
    convert_element_type x1 -> x0, other arithmetic: 4.3 us -> none  [local_block(): ((x_f32 - mean_row) * lax.rsqrt(var_row + LN_EPS) * gamma_loc).astype(jnp...]
  transfers between devices with their start and end apart: 4 -> 0, of which waited for: 4 -> 0; matrix products, arithmetic and copies ran while one was open for 14% -> 0% of each run, Pallas kernels for 0% -> 0%
where the time goes in v1:
time: 164 us
  Pallas kernels  159 us (97%)
  local copies, waits for them, and re-layouts  4.64 us (3%)
    pallas_call x1, Pallas kernels, local_block(): pl.pallas_call(kernel, out_shape=(jax.ShapeDtypeStruct((TOK, HALF), BF16)...  159 us
    unnamed x1, local copies, waits for them, and re-layouts  4.64 us

profile of v1, /device:TPU:0, one launch (start us, length us, event | category | flops | bytes accessed | tf_op | source)
XLA Modules:
  0.0 163.9 jit_solution(3736352717002760877)
XLA Ops:
  0.0 159.3 %shard_map.46 = (bf16[2048,1024]{1,0:T(8,128)(2,1)}, bf16[32,4,4,4,32,256]{5,4,3,2,1,0:T(8,128)(2,1)}) custom-call(bf16[2048,1024]{1,0:T(8,128)(2,1)} %x_ref.1, f32[1,1024]{1,0:T(1,128)} %bitcast.1, bf16[32,4096]{1,0:T(8,128)(2,1)} %w1_ref.1, bf16[128,1024]{1,0:T(8,128)(2,1)} %w2_ref.1), custom_call_target="tpu_custom_call" | custom-call | tf_op jit(solution)/shard_map/pallas_call | solution.py:273
  159.3 4.6 %copy.6 = bf16[2048,1024]{1,0:T(8,128)(2,1)} copy(bf16[2048,1024]{1,0:T(8,128)(2,1)} %get-tuple-element.6) | data formatting | bytes 8388608

commit v2 on v0

v2 whole, which is shorter than its diff:
```python
import functools

import jax
import jax.numpy as jnp
from jax import lax
from jax.experimental import pallas as pl
from jax.experimental.pallas import tpu as pltpu
from jax.sharding import PartitionSpec as P

LN_EPS = 1e-5
GELU_C = 0.7978845608028654
MESH = pl.DeviceIdType.MESH
BF16 = jnp.bfloat16
F32 = jnp.float32

NU = 32
NH = 16
UR, UC = 32, 256
ORDERS = (("x", "y", "z"), ("y", "z", "x"), ("z", "x", "y"))
FIRST_UNIT = (0, 1) + tuple(range(2, 29, 3)) + (29, 30, 31)
NB = len(FIRST_UNIT)
B0, B1 = 2, 11
SHARED = {0: 0, 1: 1, 11: 2, 12: 0, 13: 1}
EARLY = 3
TOK = 2048
DM = 2048
HALF = 1024
MT = 1024
SLOTS = 4


def gelu(a):
    return 0.5 * a * (1.0 + jnp.tanh(GELU_C * (a + 0.044715 * (a * a * a))))


def kernel(x_ref, g_ref, w1_ref, w2_ref, y_ref, w_ref, z, h, wbuf, wsh, s1, perm, gbuf, acc, xres,
           first_sem, recv_sem, send_sem, h_recv, h_send, load_sem, loc_sem, x_recv, x_send, io_sem):
    me = lax.axis_index("row")
    c = lax.axis_index("col")
    pos = {"x": lax.rem(me, 4), "y": lax.rem(me // 4, 4), "z": me // 16}
    stride = {"x": 1, "y": 4, "z": 16}

    def shifted(d, k):
        return lax.rem(pos[d] + (k + 4), 4)

    peer = {(d, k): me + (shifted(d, k) - pos[d]) * stride[d] for d in "xyz" for k in (1, -1)}

    def parts(b):
        if isinstance(b, int) and b in SHARED:
            out, at = [None] * 3, UR // 2
            for p in range(3):
                if p == SHARED[b]:
                    out[p] = (FIRST_UNIT[b], 0, UR // 2)
                else:
                    out[p] = (FIRST_UNIT[b], at, UR // 4)
                    at += UR // 4
            return out
        return [(3 * b - 4 + p, 0, UR) for p in range(3)]

    def units(b):
        if isinstance(b, int) and b in SHARED:
            return FIRST_UNIT[b], 1
        return 3 * b - 4, 3

    def region(part, p, k, at, half):
        u, r0, nr = part
        dims = ORDERS[p]
        idx = {}
        for j, d in enumerate(dims):
            idx[d] = pl.ds(0, 4) if j < k else (at if j == k else pos[d])
        cols = pl.ds(0, UC)
        if half is not None:
            if k == 0:
                cols = pl.ds(half * (UC // 2), UC // 2)
            else:
                d = [d for d in "zyx" if d in dims[:k]][0]
                idx[d] = pl.ds(2 * half, 2)
        return w_ref.at[u, idx["z"], idx["y"], idx["x"], pl.ds(r0, nr), cols]

    def bytes_of(u, k, n):
        z_, y_, x_ = [(0, 0, pl.ds(0, n)), (0, pl.ds(0, n), pl.ds(0, 4)), (pl.ds(0, n), pl.ds(0, 4), pl.ds(0, 4))][k]
        return w_ref.at[u, z_, y_, x_]

    def arrived(b, k, sub):
        if k == 0:
            return first_sem.at[0 if b < EARLY else 1, sub]
        return recv_sem.at[b, k - 1, sub]

    def send(b, part, p, k, sub, way):
        d = ORDERS[p][k]
        if sub == 0:
            dst = region(part, p, k, pos[d], None)
            src = wsh.at[part[0], pl.ds(part[1], part[2])] if k == 0 else dst
        else:
            dst = region(part, p, k, shifted(d, -way), 0 if way == 1 else 1)
            src = dst
        pltpu.make_async_remote_copy(
            src_ref=src, dst_ref=dst, send_sem=send_sem.at[k], recv_sem=arrived(b, k, sub),
            device_id={"row": peer[d, way]}, device_id_type=MESH).start()

    def when(cond, f):
        if isinstance(cond, bool):
            if cond:
                f()
        else:
            pl.when(cond)(f)

    def on_batch(b, f, single=tuple(range(B1, NB))):
        if isinstance(b, int):
            if 0 <= b < NB:
                f(b)
            return
        pl.when(jnp.logical_and(b >= B0, b < B1))(functools.partial(f, b))
        for t in single:
            pl.when(b == t)(functools.partial(f, t))

    def issue(b, k, sub):
        def f(b):
            for p, part in enumerate(parts(b)):
                send(b, part, p, k, sub, 1)
                send(b, part, p, k, sub, -1)
        on_batch(b, f)

    def take(v, sem):
        pltpu.make_async_copy(v, v, sem).wait()

    def await_(b, k, sub):
        on_batch(b, lambda b: take(bytes_of(pl.ds(*units(b)), k, 2 if sub == 0 else 1), arrived(b, k, sub)))

    def await_first(g, sub):
        u = FIRST_UNIT[EARLY]
        us = pl.ds(0, u) if g == 0 else pl.ds(u, NU - u)
        take(bytes_of(us, 0, 2 if sub == 0 else 1), first_sem.at[g, sub])

    cp_w1 = pltpu.make_async_copy(w1_ref, s1, io_sem.at[0])
    cp_w1.start()
    cp_w2 = [pltpu.make_async_copy(w2_ref.at[pl.ds(UR * rg, UR), pl.ds(UC * cg, UC)], wsh.at[NH + 4 * cg + rg], io_sem.at[1])
             for cg in range(4) for rg in range(4)]
    for cp in cp_w2:
        cp.start()
    mine = pl.ds(pl.multiple_of(c * HALF, HALF), HALF)
    cp_x = pltpu.make_async_copy(x_ref, z.at[:, mine], io_sem.at[2])
    cp_x.start()
    cp_g = pltpu.make_async_copy(g_ref, gbuf.at[c], io_sem.at[3])
    cp_g.start()

    barrier = pltpu.get_barrier_semaphore()
    for t in peer.values():
        pl.semaphore_signal(barrier, inc=1, device_id={"row": t}, device_id_type=MESH)
    pl.semaphore_signal(barrier, inc=1, device_id={"col": 1 - c}, device_id_type=MESH)

    ri = lax.broadcasted_iota(jnp.int32, (512, 512), 0)
    ci = lax.broadcasted_iota(jnp.int32, (512, 512), 1)
    want = ((ci // 32) % 4) * 128 + (ci // 128) * 32 + ci % 32
    perm[...] = jnp.where(ri == want, 1.0, 0.0).astype(BF16)
    cp_w1.wait()
    for g in range(8):
        r = jnp.dot(s1[:, g * 512:(g + 1) * 512], perm[...], preferred_element_type=F32).astype(BF16)
        for rg in range(4):
            wsh[4 * rg + g // 2, :, (g % 2) * 128:(g % 2) * 128 + 128] = r[:, rg * 128:(rg + 1) * 128]
    pl.semaphore_wait(barrier, 7)

    other = {"col": 1 - c}
    rx = pltpu.make_async_remote_copy(src_ref=x_ref, dst_ref=z.at[:, mine], send_sem=x_send.at[0], recv_sem=x_recv.at[0],
                                      device_id=other, device_id_type=MESH)
    rg_ = pltpu.make_async_remote_copy(src_ref=g_ref, dst_ref=gbuf.at[c], send_sem=x_send.at[1], recv_sem=x_recv.at[1],
                                       device_id=other, device_id_type=MESH)
    take(wsh.at[pl.ds(NH, NH)], io_sem.at[1])
    for b in range(NB):
        issue(b, 0, 0)
    own = pltpu.make_async_copy(wsh, w_ref.at[:, pos["z"], pos["y"], pos["x"]], loc_sem)
    own.start()
    await_first(0, 0)
    for b in range(EARLY):
        issue(b, 0, 1)
    rx.start()
    rg_.start()
    await_first(1, 0)
    for b in range(EARLY, NB):
        issue(b, 0, 1)
    own.wait()
    await_first(0, 1)
    for b in range(EARLY):
        issue(b, 1, 0)
    await_first(1, 1)
    for b in range(EARLY, 5):
        issue(b, 1, 0)
    for b in range(3):
        await_(b, 1, 0)
        issue(b, 1, 1)
    for b in range(2):
        await_(b, 1, 1)
        issue(b, 2, 0)

    def norm(i):
        rows = pl.ds(pl.multiple_of(i * 128, 128), 128)
        a = z[rows, :].astype(F32)
        mean = jnp.sum(a, axis=1, keepdims=True) / DM
        var = jnp.sum(a * a, axis=1, keepdims=True) / DM - mean * mean
        rs = lax.rsqrt(var + LN_EPS)
        for hf in range(2):
            cols = slice(hf * HALF, (hf + 1) * HALF)
            z[rows, cols] = ((a[:, cols] - mean) * rs * gbuf[hf]).astype(BF16)

    def load(u):
        return pltpu.make_async_copy(w_ref.at[u], wbuf.at[lax.rem(u, SLOTS)], load_sem.at[lax.rem(u, SLOTS)])

    def h_copy(u):
        cols = pl.ds(pl.multiple_of(c * HALF + lax.rem(u, 4) * UC, UC), UC)
        v = h.at[u // 4, :, cols]
        return pltpu.make_async_remote_copy(src_ref=v, dst_ref=v, send_sem=h_send, recv_sem=h_recv.at[u],
                                            device_id=other, device_id_type=MESH)

    def res_copy(cg):
        return pltpu.make_async_copy(x_ref.at[:, pl.ds(pl.multiple_of(cg * UC, UC), UC)], xres, io_sem.at[5])

    def product(lhs, slot, m):
        return jnp.dot(lhs[m * MT:(m + 1) * MT, :], wbuf[slot].reshape(DM, UC), preferred_element_type=F32)

    def gelu_unit(u):
        cols = pl.ds(pl.multiple_of(c * HALF + lax.rem(u, 4) * UC, UC), UC)
        for m in range(TOK // MT):
            h[u // 4, m * MT:(m + 1) * MT, cols] = gelu(product(z, lax.rem(u, SLOTS), m)).astype(BF16)
        h_copy(u).start()

    def acc_unit(u):
        cg = (u - NH) // 4
        rg = lax.rem(u, 4)

        def first():
            acc[...] = jnp.zeros_like(acc)
            res_copy(cg).start()

        def partner():
            for q in range(4):
                h_copy(4 * rg + q).wait_recv()

        def last():
            res_copy(cg).wait()
            y_ref[:, pl.ds(pl.multiple_of(cg * UC, UC), UC)] = (xres[...].astype(F32) + acc[...]).astype(BF16)

        when(rg == 0, first)
        when(cg == 0, partner)
        for m in range(TOK // MT):
            acc[m * MT:(m + 1) * MT, :] += product(h.at[rg], lax.rem(u, SLOTS), m)
        when(rg == 3, last)

    def head(b):
        await_(b, 2, 0)
        issue(b, 2, 1)
        await_(b + 3, 1, 0)
        issue(b + 3, 1, 1)
        issue(b + 5, 1, 0)

    def fetch(b):
        def f(b):
            u, n = units(b)
            take(bytes_of(pl.ds(u, n), 2, 1), arrived(b, 2, 1))
            for i in range(n):
                load(u + i).start()
        on_batch(b, f, (1, B1, B1 + 1))

    def mid(b):
        fetch(b - 1)
        await_(b + 2, 1, 1)
        issue(b + 2, 2, 0)

    cp_x.wait()
    cp_g.wait()
    rx.wait_recv()
    rg_.wait_recv()
    pl.loop(0, 5)(norm)
    head(0)
    mid(0)
    pl.loop(5, 16)(norm)
    head(1)
    mid(1)

    @pl.loop(B0, B1 + 1)
    def _(b):
        head(b)

        @pl.loop(0, 3)
        def _(j):
            at = 3 * b - 9 + j
            u = jnp.where(at == -1, 0, at)
            live = jnp.logical_or(at == -1, at >= 1)
            pl.when(j == 1)(functools.partial(mid, b))

            @pl.when(live)
            def _():
                load(u).wait()

            @pl.when(jnp.logical_and(live, u < NH))
            def _():
                gelu_unit(u)

            @pl.when(jnp.logical_and(live, u >= NH))
            def _():
                acc_unit(u)

    @pl.loop(NU - 5, NU)
    def _(u):
        pl.when(u == 27)(lambda: head(12))
        pl.when(u == 28)(lambda: mid(12))

        @pl.when(u == 29)
        def _():
            head(13)
            mid(13)

        pl.when(u == 30)(lambda: fetch(13))
        load(u).wait()
        acc_unit(u)

    rx.wait_send()
    rg_.wait_send()
    take(h.at[pl.ds(0, 2)], h_send)
    for k in range(3):
        take(bytes_of(pl.ds(0, NU), k, 3), send_sem.at[k])


def solution(mesh):
    tok_spec = P(("dp", "row"), "col")

    def local_block(x_loc, gamma_loc, w_in_loc, w_out_loc):
        y, _ = pl.pallas_call(
            kernel,
            out_shape=(pltpu.VMEM((TOK, HALF), BF16), jax.ShapeDtypeStruct((NU, 4, 4, 4, UR, UC), BF16)),
            in_specs=[pl.BlockSpec(memory_space=pl.ANY)] * 4,
            out_specs=(pl.BlockSpec(memory_space=pltpu.VMEM), pl.BlockSpec(memory_space=pl.ANY)),
            scratch_shapes=[
                pltpu.VMEM((TOK, DM), BF16),
                pltpu.VMEM((4, TOK, DM), BF16),
                pltpu.VMEM((SLOTS, 4, 4, 4, UR, UC), BF16),
                pltpu.VMEM((NU, UR, UC), BF16),
                pltpu.VMEM((UR, 4096), BF16),
                pltpu.VMEM((512, 512), BF16),
                pltpu.VMEM((2, 1, HALF), F32),
                pltpu.VMEM((TOK, UC), F32),
                pltpu.VMEM((TOK, UC), BF16),
                pltpu.SemaphoreType.DMA((2, 2)),
                pltpu.SemaphoreType.DMA((NB, 2, 2)),
                pltpu.SemaphoreType.DMA((3,)),
                pltpu.SemaphoreType.DMA((NH,)),
                pltpu.SemaphoreType.DMA,
                pltpu.SemaphoreType.DMA((SLOTS,)),
                pltpu.SemaphoreType.DMA,
                pltpu.SemaphoreType.DMA((2,)),
                pltpu.SemaphoreType.DMA((2,)),
                pltpu.SemaphoreType.DMA((6,)),
            ],
            compiler_params=pltpu.CompilerParams(collective_id=0, has_side_effects=True, vmem_limit_bytes=57 * 1024 * 1024),
        )(x_loc, gamma_loc.reshape(1, HALF), w_in_loc, w_out_loc)
        return y

    return jax.shard_map(local_block, mesh=mesh, in_specs=(tok_spec, P("col"), P("row", "col"), P("row", "col")), out_specs=tok_spec, check_vma=False)
```

time: 366 us -> 151 us (0.41)
  waiting for transfers between devices: 245 us -> 0 us
  Pallas kernels: 0 us -> 149 us
  matrix products: 94.5 us -> 0 us
  between operations: 13.1 us -> 0.01 us
  other arithmetic: 7.78 us -> 0 us
    all_gather x4 -> x0, waiting for transfers between devices: 244 us -> none  [the longest x1 108 us: local_block(): w_in_panel = lax.all_gather(w_in_loc, 'row', axis=0, tiled=True)]
    pallas_call x0 -> x1, Pallas kernels: none -> 149 us  [local_block(): pl.pallas_call(kernel, out_shape=(pltpu.VMEM((TOK, HALF), BF16), jax.Shap...]
    dot_general x2 -> x0, matrix products: 94.5 us -> none  [the longest x1 49.8 us: local_block(): pre_act = jnp.dot(z_panel, w_in_panel, preferred_element_type=jnp.float32)]
    convert_element_type x1 -> x0, other arithmetic: 4.3 us -> none  [local_block(): ((x_f32 - mean_row) * lax.rsqrt(var_row + LN_EPS) * gamma_loc).astype(jnp...]
  transfers between devices with their start and end apart: 4 -> 0, of which waited for: 4 -> 0; matrix products, arithmetic and copies ran while one was open for 14% -> 0% of each run, Pallas kernels for 0% -> 0%
where the time goes in v2:
time: 151 us
  Pallas kernels  149 us (99%)
  local copies, waits for them, and re-layouts  2.02 us (1%)
    pallas_call x1, Pallas kernels, local_block(): pl.pallas_call(kernel, out_shape=(pltpu.VMEM((TOK, HALF), BF16), jax.Shap...  149 us

profile of v2, /device:TPU:0, one launch (start us, length us, event | category | flops | bytes accessed | tf_op | source)
XLA Modules:
  0.0 150.8 jit_solution(3357229972187556065)
XLA Ops:
  0.0 148.8 %shard_map.46 = (bf16[2048,1024]{1,0:T(8,128)(2,1)S(1)}, bf16[32,4,4,4,32,256]{5,4,3,2,1,0:T(8,128)(2,1)}) custom-call(bf16[2048,1024]{1,0:T(8,128)(2,1)} %x_ref.1, f32[1,1024]{1,0:T(1,128)} %bitcast.1, bf16[32,4096]{1,0:T(8,128)(2,1)} %w1_ref.1, bf16[128,1024]{1,0:T(8,128)(2,1)} %w2_ref.1), custom_call_target="tpu_custom_call" | custom-call | tf_op jit(solution)/shard_map/pallas_call | solution.py:327
  148.8 2.0 %copy.6 = bf16[2048,1024]{1,0:T(8,128)(2,1)} copy(bf16[2048,1024]{1,0:T(8,128)(2,1)S(1)} %get-tuple-element.6) | data formatting | bytes 8388608
